TPU v7x, 32 devices: a whole 2x2x4 slice. The times are simulated.
32 devices in a mesh: row: 2 (over y), col: 8 (over z, x), rep: 2 (over core).
Axes of the slice: x: 2, y: 2, z: 4, core: 2. Of those that a mesh axis runs over, the one named last changes fastest.
Arguments:
- gain: float32 [48, 8, 128, 128], P(('row', 'col'), 'rep'), as said below
- coupled_columns: int32 [48, 8], P(('row', 'col')), may hold values from 0 to 47, as said below
- solution: float32 [6144, 512], P(('row', 'col')), may hold values from -6 to 6
- residual: float32 [6144, 512], P(('row', 'col')), may hold values from -6 to 6
- direction: float32 [6144, 512], P(('row', 'col')), may hold values from -6 to 6
Outputs:
- solution_next: float32 [6144, 512], P(('row', 'col'))
- residual_next: float32 [6144, 512], P(('row', 'col'))
- direction_next: float32 [6144, 512], P(('row', 'col'))
Inputs may be any that keep to these rules, and one draw needn't show every extreme that they name: `coupled_columns`: each block row i names first its coupled block columns in ascending order (always i - 1, i, i + 1 where inside 0 to 47, some of i - 3, i - 2, i + 2, i + 3, the coupling being symmetric), at most 7 of them, and then fills the remaining slots with i itself; every named column is within 3 of i. The gain matrix assembled from its blocks is symmetric; padding slots hold zero blocks; each diagonal entry exceeds the sum of the absolute values of the other entries of its row by exactly 1.
All inputs are finite; a program needn't handle non-finite values.
Results may differ from a plain program's by a relative error of at most 0.000061.
Values sent between devices are 32-bit elements; how exact they have to be, the bound alone decides.
A program may use at most 64 MiB of HBM per device.

v0:
```python
import jax
import jax.numpy as jnp
from jax import lax
from jax.sharding import PartitionSpec as P

BLK = 128
reach_blocks = 3


def extended_2(block, sides, width):
    for axis, dim in sides:
        count = lax.axis_size(axis)
        forward = [(i, i + 1) for i in range(count - 1)]
        backward = [(target, source) for source, target in forward]
        low = lax.ppermute(
            lax.slice_in_dim(block, block.shape[dim] - width, None, axis=dim), axis, forward
        )
        high = lax.ppermute(lax.slice_in_dim(block, 0, width, axis=dim), axis, backward)
        block = jnp.concatenate([low, block, high], axis=dim)
    return block


def per_device(gain, coupled_columns, solution, residual, direction):
    row_blocks = coupled_columns.shape[0]
    snapshots = direction.shape[1]
    first_block = lax.axis_index(("row", "col")) * row_blocks
    extended = extended_2(direction, ((("row", "col"), 0),), reach_blocks * BLK)
    segments = extended.reshape(row_blocks + 2 * reach_blocks, BLK, snapshots)
    half_slots = gain.shape[1]
    own_columns = lax.dynamic_slice_in_dim(
        coupled_columns, lax.axis_index("rep") * half_slots, half_slots, 1
    )
    local_index = own_columns - first_block + reach_blocks
    picked = segments[local_index]
    product = jnp.einsum(
        "rkab,rkbs->ras",
        gain,
        picked,
        precision=lax.Precision.HIGHEST,
        preferred_element_type=jnp.float32,
    )
    image = lax.psum(product.reshape(row_blocks * BLK, snapshots), "rep")
    norm_old, curvature, crossing, image_square = lax.psum(
        (
            jnp.sum(residual * residual, axis=0),
            jnp.sum(direction * image, axis=0),
            jnp.sum(residual * image, axis=0),
            jnp.sum(image * image, axis=0),
        ),
        ("row", "col"),
    )
    step_size = norm_old / curvature
    solution_next = solution + step_size * direction
    residual_next = residual - step_size * image
    norm_new = norm_old - 2.0 * step_size * crossing + step_size * step_size * image_square
    direction_next = residual_next + norm_new / norm_old * direction
    return (solution_next, residual_next, direction_next)


def solution(mesh):
    return jax.shard_map(
        per_device,
        mesh=mesh,
        in_specs=(
            P(("row", "col"), "rep", None, None),
            P(("row", "col"), None),
            P(("row", "col"), None),
            P(("row", "col"), None),
            P(("row", "col"), None),
        ),
        out_specs=(P(("row", "col"), None), P(("row", "col"), None), P(("row", "col"), None)),
        check_vma=False,
    )
```

profile of v0, /device:TPU:0, one launch (start us, length us, event | category | flops | bytes accessed | tf_op | source)
XLA Modules:
  0.0 132.4 jit_solution(13395826707546090617)
XLA Ops:
  7.2 0.0 copy-start
  7.2 0.0 all-reduce.3.cloned.1.call-start
  7.2 1.4 %collective-permute-start.1 = (f32[384,512]{1,0:T(8,128)}, f32[384,512]{1,0:T(8,128)S(1)}, u32[]{:S(2)}, u32[]{:S(2)}) collective-permute-start(f32[384,512]{1,0:T(8,128)} %param.9), channel_id=1, source_target_pairs={{2,0},{4,2},{6,4},{8,6},{10,8},{12,10},{14,12},{16,14},{18,16},{20... | collective-permute-start | bytes 2359304 | tf_op jit(solution)/shard_map/ppermute | solution.py:18
  8.7 6.4 %collective-permute-start = (f32[384,512]{1,0:T(8,128)}, f32[384,512]{1,0:T(8,128)}, u32[]{:S(2)}, u32[]{:S(2)}) collective-permute-start(f32[384,512]{1,0:T(8,128)} %param.9), channel_id=1, source_target_pairs={{0,2},{2,4},{4,6},{6,8},{8,10},{10,12},{12,14},{14,16},{16,18},{18... | collective-permute-start | bytes 2359304 | tf_op jit(solution)/shard_map/ppermute | solution.py:15
  15.0 0.8 compare_select_fusion
  15.8 0.1 reshape.18
  15.9 30.9 %collective-permute-done.1 = f32[384,512]{1,0:T(8,128)S(1)} collective-permute-done((f32[384,512]{1,0:T(8,128)}, f32[384,512]{1,0:T(8,128)S(1)}, u32[]{:S(2)}, u32[]{:S(2)}) %collective-permute-start.1) | collective-permute-done | bytes 786464 | tf_op jit(solution)/shard_map/ppermute | solution.py:18
  46.8 0.0 copy-start.4
  46.8 0.9 copy-done.4
  47.7 0.0 collective-permute-done
  47.7 1.8 %pad_maximum_fusion = f32[1152,512]{1,0:T(8,128)S(1)} fusion(f32[384,512]{1,0:T(8,128)} %copy-done.4, f32[384,512]{1,0:T(8,128)} %param.9, f32[384,512]{1,0:T(8,128)} %collective-permute-done), kind=kLoop, calls=%fused_computation.1 | loop fusion | flops 1179648 | bytes 4718592 | tf_op jit(solution)/shard_map/concatenate | solution.py:19
  49.5 2.4 %gather_fusion = f32[12,128,512]{2,1,0:T(8,128)} fusion(f32[9,128,512]{2,1,0:T(8,128)S(1)} %bitcast.10, s32[1024]{0:T(1024)S(1)} %pad_clamp_fusion), kind=kCustom, calls=%fused_computation | custom fusion | bytes 6291504 | tf_op jit(solution)/shard_map/gather | solution.py:34
  51.9 0.0 copy-start.1
  51.9 0.0 copy-start.2
  51.9 0.0 copy-done
  52.0 0.0 copy-start.3
  52.0 4.8 %fusion = f32[3,512,128,1]{1,2,3,0:T(8,128)} fusion(f32[3,4,128,512]{3,2,1,0:T(8,128)} %bitcast.11, f32[3,4,128,128]{3,2,1,0:T(8,128)S(1)} %copy-done), kind=kOutput, calls=%fused_computation.12 | convolution fusion | flops 1207959552 | bytes 4718592 | tf_op jit(solution)/shard_map/rkab,rkbs->ras/dot_general | solution.py:35
  56.7 0.0 all-reduce.3.cloned.1.call-update
  56.7 22.1 %all-reduce.3.cloned.1.call-done = f32[384,512]{1,0:T(8,128)} async-done(((f32[384,512]{1,0:T(8,128)}), f32[384,512]{1,0:T(8,128)}) %all-reduce.3.cloned.1.call-update) | async-done | bytes 786448 | tf_op jit(solution)/shard_map/psum | solution.py:42
  78.8 0.0 copy-done.1
  78.8 0.0 copy-done.2
  78.8 1.4 %multiply_reduce_fusion.1 = (f32[512]{0:T(512)S(1)}, f32[512]{0:T(512)S(1)}, f32[512]{0:T(512)S(1)}, f32[512]{0:T(512)S(1)}) fusion(f32[384,512]{1,0:T(8,128)S(1)} %copy-done.2, f32[384,512]{1,0:T(8,128)} %all-reduce.3.cloned.1.call-done, f32[384,512]{1,0:T(8,128)S(1)} %copy-done.1), kind=kLoop, calls=%fused_computation.4 | loop fusion | flops 1570816 | bytes 2367488 | tf_op jit(solution)/shard_map/reduce_sum | solution.py:47
  80.2 42.5 %all-reduce = (f32[512]{0:T(512)S(1)}, f32[512]{0:T(512)S(1)}, f32[512]{0:T(512)S(1)}, f32[512]{0:T(512)S(1)}) all-reduce(f32[512]{0:T(512)S(1)} %get-tuple-element.6, f32[512]{0:T(512)S(1)} %get-tuple-element.5, f32[512]{0:T(512)S(1)} %get-tuple-element.4, ...), channel_id=1, replica_groups=mesh['row'=2,'col'=8,'rep'=2] {'row','col'}, use_global_device_ids=true, to_apply=%region_1.0 | all-reduce | flops 2048 | bytes 16384 | tf_op jit(solution)/shard_map/psum | solution.py:43
  122.8 0.0 copy-done.3
  122.8 2.8 %multiply_add_fusion = (f32[384,512]{1,0:T(8,128)}, f32[384,512]{1,0:T(8,128)}, f32[384,512]{1,0:T(8,128)}) fusion(f32[384,512]{1,0:T(8,128)S(1)} %copy-done.1, f32[512]{0:T(512)S(1)} %get-tuple-element.13, f32[384,512]{1,0:T(8,128)S(1)} %copy-done.2, f32[384,512]{1,0:T(8,128)} %all-reduce.3.cloned.1.call-done, f32[512]{0:T(512)S(1)} %get-tuple-element.14, ...), kind=kLoop, calls=%fused_computation.2 | loop fusion | flops 1179648 | bytes 5509120 | tf_op jit(solution)/shard_map/add | solution.py:56
  (2 shorter events, 0.0 us)
Async XLA Ops:
  7.2 44.8 %copy-start = (f32[3,4,128,128]{3,2,1,0:T(8,128)S(1)}, f32[3,4,128,128]{3,2,1,0:T(8,128)}, u32[]{:S(2)}) copy-start(f32[3,4,128,128]{3,2,1,0:T(8,128)} %param.5) | copy-start | bytes 2359300
  7.2 71.6 %all-reduce.3.cloned.1.call-start = ((), (), s32[]{:S(2)}) async-start(), calls=%async_computation | async-start | bytes 1572864 | tf_op jit(solution)/shard_map/psum | solution.py:42
  7.2 39.6 %collective-permute-start.1 = (f32[384,512]{1,0:T(8,128)}, f32[384,512]{1,0:T(8,128)S(1)}, u32[]{:S(2)}, u32[]{:S(2)}) collective-permute-start(f32[384,512]{1,0:T(8,128)} %param.9), channel_id=1, source_target_pairs={{2,0},{4,2},{6,4},{8,6},{10,8},{12,10},{14,12},{16,14},{18,16},{20... | collective-permute-start | bytes 2359304 | tf_op jit(solution)/shard_map/ppermute | solution.py:18
  8.7 39.1 %collective-permute-start = (f32[384,512]{1,0:T(8,128)}, f32[384,512]{1,0:T(8,128)}, u32[]{:S(2)}, u32[]{:S(2)}) collective-permute-start(f32[384,512]{1,0:T(8,128)} %param.9), channel_id=1, source_target_pairs={{0,2},{2,4},{4,6},{6,8},{8,10},{10,12},{12,14},{14,16},{16,18},{18... | collective-permute-start | bytes 2359304 | tf_op jit(solution)/shard_map/ppermute | solution.py:15
  46.8 0.9 copy-start.4
  51.9 26.9 %copy-start.1 = (f32[384,512]{1,0:T(8,128)S(1)}, f32[384,512]{1,0:T(8,128)}, u32[]{:S(2)}) copy-start(f32[384,512]{1,0:T(8,128)} %param.9) | copy-start | bytes 2359300
  51.9 26.9 %copy-start.2 = (f32[384,512]{1,0:T(8,128)S(1)}, f32[384,512]{1,0:T(8,128)}, u32[]{:S(2)}) copy-start(f32[384,512]{1,0:T(8,128)} %param.8) | copy-start | bytes 2359300
  52.0 70.8 %copy-start.3 = (f32[384,512]{1,0:T(8,128)S(1)}, f32[384,512]{1,0:T(8,128)}, u32[]{:S(2)}) copy-start(f32[384,512]{1,0:T(8,128)} %param.7) | copy-start | bytes 2359300
Sparse Core Ops, SparseCore 0:
  56.9 21.8 all-reduce.2
where the time goes:
time: 133 us; the launch traced here: 132 us
  waiting for transfers between devices  53 us (40%)
  blocking collectives  42.5 us (32%)
  between operations  14.1 us (11%)
  starting transfers between devices  7.85 us (6%)
  other arithmetic  6.84 us (5%)
  matrix products  4.76 us (4%)
  local copies, waits for them, and re-layouts  3.4 us (3%)
    psum x1, blocking collectives, per_device(): lax.psum((jnp.sum(residual * residual, axis=0), jnp.sum(direction * image...  42.5 us
    ppermute x1, waiting for transfers between devices, extended_2(): lax.ppermute(lax.slice_in_dim(block, 0, width, axis=dim), axis, backward)  30.9 us
    psum x1, waiting for transfers between devices, per_device(): image = lax.psum(product.reshape(row_blocks * BLK, snapshots), 'rep')  22.1 us
    ppermute x1, starting transfers between devices, extended_2(): lax.ppermute(lax.slice_in_dim(block, block.shape[dim] - width, None, axis...  6.39 us
    dot_general x1, matrix products, per_device(): jnp.einsum('rkab,rkbs->ras', gain, picked, precision=lax.Precision.HIGHES...  4.76 us
    add x1, other arithmetic, per_device(): direction_next = residual_next + norm_new / norm_old * direction  2.82 us
  transfers between devices with their start and end apart: 3, of which 2 were waited for; matrix products, arithmetic and copies ran while one was open for 1% of the time, Pallas kernels for 0%

commit v1 on v0

--- a/solution.py
+++ b/solution.py
@@ -41,13 +41,16 @@
     )
     image = lax.psum(product.reshape(row_blocks * BLK, snapshots), "rep")
     norm_old, curvature, crossing, image_square = lax.psum(
-        (
-            jnp.sum(residual * residual, axis=0),
-            jnp.sum(direction * image, axis=0),
-            jnp.sum(residual * image, axis=0),
-            jnp.sum(image * image, axis=0),
+        lax.psum(
+            (
+                jnp.sum(residual * residual, axis=0),
+                jnp.sum(direction * image, axis=0),
+                jnp.sum(residual * image, axis=0),
+                jnp.sum(image * image, axis=0),
+            ),
+            "col",
         ),
-        ("row", "col"),
+        "row",
     )
     step_size = norm_old / curvature
     solution_next = solution + step_size * direction

time: 133 us -> 117 us (0.88)
  blocking collectives: 42.5 us -> 26.9 us
    psum x1, blocking collectives: 42.5 us -> 21.9 us  [per_device(): lax.psum((jnp.sum(residual * residual, axis=0), jnp.sum(direction * image...]
    psum x0 -> x1, blocking collectives: none -> 4.99 us  [per_device(): lax.psum(lax.psum((jnp.sum(residual * residual, axis=0), jnp.sum(directio...]
where the time goes in v1:
time: 117 us
  waiting for transfers between devices  53 us (45%)
  blocking collectives  26.9 us (23%)
  between operations  14.1 us (12%)
  starting transfers between devices  7.85 us (7%)
  other arithmetic  6.84 us (6%)
  matrix products  4.76 us (4%)
  local copies, waits for them, and re-layouts  3.4 us (3%)
    ppermute x1, waiting for transfers between devices, extended_2(): lax.ppermute(lax.slice_in_dim(block, 0, width, axis=dim), axis, backward)  30.9 us
    psum x1, waiting for transfers between devices, per_device(): image = lax.psum(product.reshape(row_blocks * BLK, snapshots), 'rep')  22.1 us
    psum x1, blocking collectives, per_device(): lax.psum((jnp.sum(residual * residual, axis=0), jnp.sum(direction * image...  21.9 us
    ppermute x1, starting transfers between devices, extended_2(): lax.ppermute(lax.slice_in_dim(block, block.shape[dim] - width, None, axis...  6.39 us
    psum x1, blocking collectives, per_device(): lax.psum(lax.psum((jnp.sum(residual * residual, axis=0), jnp.sum(directio...  4.99 us
    dot_general x1, matrix products, per_device(): jnp.einsum('rkab,rkbs->ras', gain, picked, precision=lax.Precision.HIGHES...  4.76 us
    add x1, other arithmetic, per_device(): direction_next = residual_next + norm_new / norm_old * direction  2.82 us
    gather x1, local copies, waits for them, and re-layouts, per_device(): picked = segments[local_index]  2.42 us
  transfers between devices with their start and end apart: 3, of which 2 were waited for; matrix products, arithmetic and copies ran while one was open for 1% of the time, Pallas kernels for 0%

profile of v1, /device:TPU:0, one launch (start us, length us, event | category | flops | bytes accessed | tf_op | source)
XLA Modules:
  0.0 116.8 jit_solution(18411321871543987486)
XLA Ops:
  7.2 0.0 copy-start
  7.2 0.0 all-reduce.4.cloned.1.call-start
  7.2 1.4 %collective-permute-start.1 = (f32[384,512]{1,0:T(8,128)}, f32[384,512]{1,0:T(8,128)S(1)}, u32[]{:S(2)}, u32[]{:S(2)}) collective-permute-start(f32[384,512]{1,0:T(8,128)} %param.9), channel_id=1, source_target_pairs={{2,0},{4,2},{6,4},{8,6},{10,8},{12,10},{14,12},{16,14},{18,16},{20... | collective-permute-start | bytes 2359304 | tf_op jit(solution)/shard_map/ppermute | solution.py:18
  8.7 6.4 %collective-permute-start = (f32[384,512]{1,0:T(8,128)}, f32[384,512]{1,0:T(8,128)}, u32[]{:S(2)}, u32[]{:S(2)}) collective-permute-start(f32[384,512]{1,0:T(8,128)} %param.9), channel_id=1, source_target_pairs={{0,2},{2,4},{4,6},{6,8},{8,10},{10,12},{12,14},{14,16},{16,18},{18... | collective-permute-start | bytes 2359304 | tf_op jit(solution)/shard_map/ppermute | solution.py:15
  15.0 0.8 compare_select_fusion
  15.8 0.1 reshape.18
  15.9 30.9 %collective-permute-done.1 = f32[384,512]{1,0:T(8,128)S(1)} collective-permute-done((f32[384,512]{1,0:T(8,128)}, f32[384,512]{1,0:T(8,128)S(1)}, u32[]{:S(2)}, u32[]{:S(2)}) %collective-permute-start.1) | collective-permute-done | bytes 786464 | tf_op jit(solution)/shard_map/ppermute | solution.py:18
  46.8 0.0 copy-start.4
  46.8 0.9 copy-done.4
  47.7 0.0 collective-permute-done
  47.7 1.8 %pad_maximum_fusion = f32[1152,512]{1,0:T(8,128)S(1)} fusion(f32[384,512]{1,0:T(8,128)} %copy-done.4, f32[384,512]{1,0:T(8,128)} %param.9, f32[384,512]{1,0:T(8,128)} %collective-permute-done), kind=kLoop, calls=%fused_computation.1 | loop fusion | flops 1179648 | bytes 4718592 | tf_op jit(solution)/shard_map/concatenate | solution.py:19
  49.5 2.4 %gather_fusion = f32[12,128,512]{2,1,0:T(8,128)} fusion(f32[9,128,512]{2,1,0:T(8,128)S(1)} %bitcast.10, s32[1024]{0:T(1024)S(1)} %pad_clamp_fusion), kind=kCustom, calls=%fused_computation | custom fusion | bytes 6291504 | tf_op jit(solution)/shard_map/gather | solution.py:34
  51.9 0.0 copy-start.1
  51.9 0.0 copy-start.2
  51.9 0.0 copy-done
  52.0 0.0 copy-start.3
  52.0 4.8 %fusion = f32[3,512,128,1]{1,2,3,0:T(8,128)} fusion(f32[3,4,128,512]{3,2,1,0:T(8,128)} %bitcast.11, f32[3,4,128,128]{3,2,1,0:T(8,128)S(1)} %copy-done), kind=kOutput, calls=%fused_computation.12 | convolution fusion | flops 1207959552 | bytes 4718592 | tf_op jit(solution)/shard_map/rkab,rkbs->ras/dot_general | solution.py:35
  56.7 0.0 all-reduce.4.cloned.1.call-update
  56.7 22.1 %all-reduce.4.cloned.1.call-done = f32[384,512]{1,0:T(8,128)} async-done(((f32[384,512]{1,0:T(8,128)}), f32[384,512]{1,0:T(8,128)}) %all-reduce.4.cloned.1.call-update) | async-done | bytes 786448 | tf_op jit(solution)/shard_map/psum | solution.py:42
  78.8 0.0 copy-done.1
  78.8 0.0 copy-done.2
  78.8 1.4 %multiply_reduce_fusion.1 = (f32[512]{0:T(512)S(1)}, f32[512]{0:T(512)S(1)}, f32[512]{0:T(512)S(1)}, f32[512]{0:T(512)S(1)}) fusion(f32[384,512]{1,0:T(8,128)S(1)} %copy-done.2, f32[384,512]{1,0:T(8,128)} %all-reduce.4.cloned.1.call-done, f32[384,512]{1,0:T(8,128)S(1)} %copy-done.1), kind=kLoop, calls=%fused_computation.4 | loop fusion | flops 1570816 | bytes 2367488 | tf_op jit(solution)/shard_map/reduce_sum | solution.py:48
  80.2 21.9 %all-reduce = (f32[512]{0:T(512)S(1)}, f32[512]{0:T(512)S(1)}, f32[512]{0:T(512)S(1)}, f32[512]{0:T(512)S(1)}) all-reduce(f32[512]{0:T(512)S(1)} %get-tuple-element.6, f32[512]{0:T(512)S(1)} %get-tuple-element.5, f32[512]{0:T(512)S(1)} %get-tuple-element.4, f32[512]{0:T(512)S(1)} %get-tuple-element.3), channel_id=1, replica_groups=mesh['row'=2,'col'=8,'rep'=2] {'col'}, use_global_device_ids=true, to_apply=%region_1.0 | all-reduce | flops 2048 | bytes 16384 | tf_op jit(solution)/shard_map/psum | solution.py:44
  102.1 5.0 %all-reduce.1 = (f32[512]{0:T(512)S(1)}, f32[512]{0:T(512)S(1)}, f32[512]{0:T(512)S(1)}, f32[512]{0:T(512)S(1)}) all-reduce(f32[512]{0:T(512)S(1)} %get-tuple-element.7, f32[512]{0:T(512)S(1)} %get-tuple-element.8, f32[512]{0:T(512)S(1)} %get-tuple-element.9, ...), channel_id=1, replica_groups=mesh['row'=2,'col'=8,'rep'=2] {'row'}, use_global_device_ids=true, to_apply=%region_2.0 | all-reduce | flops 2048 | bytes 16384 | tf_op jit(solution)/shard_map/psum | solution.py:43
  107.1 0.0 copy-done.3
  107.1 2.8 %multiply_add_fusion = (f32[384,512]{1,0:T(8,128)}, f32[384,512]{1,0:T(8,128)}, f32[384,512]{1,0:T(8,128)}) fusion(f32[384,512]{1,0:T(8,128)S(1)} %copy-done.1, f32[512]{0:T(512)S(1)} %get-tuple-element.17, f32[384,512]{1,0:T(8,128)S(1)} %copy-done.2, f32[384,512]{1,0:T(8,128)} %all-reduce.4.cloned.1.call-done, f32[512]{0:T(512)S(1)} %get-tuple-element.18, ...), kind=kLoop, calls=%fused_computation.2 | loop fusion | flops 1179648 | bytes 5509120 | tf_op jit(solution)/shard_map/add | solution.py:59
  (2 shorter events, 0.0 us)
Async XLA Ops:
  7.2 44.8 %copy-start = (f32[3,4,128,128]{3,2,1,0:T(8,128)S(1)}, f32[3,4,128,128]{3,2,1,0:T(8,128)}, u32[]{:S(2)}) copy-start(f32[3,4,128,128]{3,2,1,0:T(8,128)} %param.5) | copy-start | bytes 2359300
  7.2 71.6 %all-reduce.4.cloned.1.call-start = ((), (), s32[]{:S(2)}) async-start(), calls=%async_computation | async-start | bytes 1572864 | tf_op jit(solution)/shard_map/psum | solution.py:42
  7.2 39.6 %collective-permute-start.1 = (f32[384,512]{1,0:T(8,128)}, f32[384,512]{1,0:T(8,128)S(1)}, u32[]{:S(2)}, u32[]{:S(2)}) collective-permute-start(f32[384,512]{1,0:T(8,128)} %param.9), channel_id=1, source_target_pairs={{2,0},{4,2},{6,4},{8,6},{10,8},{12,10},{14,12},{16,14},{18,16},{20... | collective-permute-start | bytes 2359304 | tf_op jit(solution)/shard_map/ppermute | solution.py:18
  8.7 39.1 %collective-permute-start = (f32[384,512]{1,0:T(8,128)}, f32[384,512]{1,0:T(8,128)}, u32[]{:S(2)}, u32[]{:S(2)}) collective-permute-start(f32[384,512]{1,0:T(8,128)} %param.9), channel_id=1, source_target_pairs={{0,2},{2,4},{4,6},{6,8},{8,10},{10,12},{12,14},{14,16},{16,18},{18... | collective-permute-start | bytes 2359304 | tf_op jit(solution)/shard_map/ppermute | solution.py:15
  46.8 0.9 copy-start.4
  51.9 26.9 %copy-start.1 = (f32[384,512]{1,0:T(8,128)S(1)}, f32[384,512]{1,0:T(8,128)}, u32[]{:S(2)}) copy-start(f32[384,512]{1,0:T(8,128)} %param.9) | copy-start | bytes 2359300
  51.9 26.9 %copy-start.2 = (f32[384,512]{1,0:T(8,128)S(1)}, f32[384,512]{1,0:T(8,128)}, u32[]{:S(2)}) copy-start(f32[384,512]{1,0:T(8,128)} %param.8) | copy-start | bytes 2359300
  52.0 55.2 %copy-start.3 = (f32[384,512]{1,0:T(8,128)S(1)}, f32[384,512]{1,0:T(8,128)}, u32[]{:S(2)}) copy-start(f32[384,512]{1,0:T(8,128)} %param.7) | copy-start | bytes 2359300
Sparse Core Ops, SparseCore 0:
  56.9 21.8 all-reduce.3
